TPU v7x, 32 devices: a whole 2x2x4 slice. The times are simulated.
32 devices in a mesh: fsdp: 8 (over y, x, core), seq: 4 (over z).
Axes of the slice: x: 2, y: 2, z: 4, core: 2. Of those that a mesh axis runs over, the one named last changes fastest.
Arguments:
- layer_input: bfloat16 [8, 512, 4096], P('fsdp', 'seq'), may hold values from -6 to 6
- dt_weight: bfloat16 [4096, 64], P('fsdp'), may hold values from -0.09375 to 0.09375
- dt_bias: float32 [64], replicated, may hold values from -2 to -0.5
- decay_rate: float32 [64], replicated, may hold values from 0.0005 to 0.25
- ssm_input: bfloat16 [8, 512, 2048], P('fsdp', 'seq'), may hold values from -6 to 6
- in_basis: bfloat16 [8, 512, 512], P('fsdp', 'seq'), may hold values from -0.59765625 to 0.59765625
- out_basis: bfloat16 [8, 512, 512], P('fsdp', 'seq'), may hold values from -0.59765625 to 0.59765625
- out_cotangent: bfloat16 [8, 512, 2048], P('fsdp', 'seq'), may hold values from -6 to 6
Outputs:
- grad_input: bfloat16 [8, 512, 2048], P('fsdp', 'seq')
- grad_in_basis: bfloat16 [8, 512, 512], P('fsdp', 'seq')
- grad_out_basis: bfloat16 [8, 512, 512], P('fsdp', 'seq')
- grad_dt_weight: float32 [4096, 64], P('fsdp')
All inputs are finite; a program needn't handle non-finite values.
Results may differ from a plain program's by a relative error of at most 0.011.
Values may be sent and summed in bfloat16 or wider, within the bound.
A program may use at most 64 MiB of HBM per device.

v0:
```python
import functools

import jax
import jax.numpy as jnp
from jax import lax
from jax.experimental import pallas as pl
from jax.experimental.pallas import tpu as pltpu
from jax.sharding import PartitionSpec as P

STATE = 128
F32 = jnp.float32
BF16 = jnp.bfloat16
MESH = pl.DeviceIdType.MESH
HIGH = lax.Precision.HIGHEST


def dot(a, b, ca=1, cb=0, precision=None):
    return lax.dot_general(
        a, b, (((ca,), (cb,)), ((), ())), precision=precision, preferred_element_type=F32
    )


def halves(value, axis):
    high = value.astype(BF16)
    low = (value - high.astype(F32)).astype(BF16)
    return jnp.concatenate([high, low], axis=axis)


def iota(shape, dim):
    return lax.broadcasted_iota(jnp.int32, shape, dim)


def kernel(
    nf,
    ns,
    tokens_hbm,
    weight_t,
    bias,
    rate_row,
    x_hbm,
    b_hbm,
    c_hbm,
    dy_hbm,
    x_out,
    b_out,
    c_out_hbm,
    out_w,
    tokens,
    x,
    b_in,
    c_out,
    dy,
    out_x,
    out_b,
    out_c,
    in_sem,
    out_sem,
    gathered,
    raw_t,
    cum_t,
    step_t,
    block_t,
    cum_g,
    step_g,
    tail_g,
    lead_g,
    state_loc,
    grad_loc,
    xs_g,
    ds_g,
    entry,
    later,
    send_f,
    send_b,
    through,
    grad_b,
    grad_c,
    col_t,
    xt_t,
    xc_t,
    ent_t,
    total,
    rs_send,
    rs_recv,
    z_recv,
    ag_ssem,
    ag_rsem,
    f_ssem,
    f_rsem,
    b_ssem,
    b_rsem,
    rs_ssem,
    rs_rsem,
    z_ssem,
    z_rsem,
):
    f = lax.axis_index("fsdp")
    z = lax.axis_index("seq")
    length = tokens.shape[0]
    heads, rows = weight_t.shape
    groups = b_in.shape[1] // STATE
    per = heads // groups
    wide = x.shape[1] // groups
    size = wide // per
    bits = nf.bit_length() - 1
    part_heads = heads // 2
    chunk = wide // 2
    loads = [
        pltpu.make_async_copy(source, target, in_sem.at[n])
        for n, (source, target) in enumerate(
            (
                (tokens_hbm, tokens),
                (x_hbm, x),
                (dy_hbm, dy),
                (b_hbm, b_in),
                (c_hbm, c_out),
            )
        )
    ]
    for load in loads:
        load.start()
    orders = (list(reversed(range(bits))), list(range(1, bits)) + [0])

    def slot_of(index, order):
        return sum(((index // 2**b) % 2) * 2**i for i, b in enumerate(order))

    def partner(j):
        return f + (1 - 2 * ((f // 2**j) % 2)) * 2**j

    barrier = pltpu.get_barrier_semaphore()
    for j in range(bits):
        pl.semaphore_signal(
            barrier, inc=1, device_id={"fsdp": partner(j)}, device_id_type=MESH
        )
    for d in range(1, ns):
        pl.semaphore_signal(
            barrier, inc=1, device_id={"seq": (z + d) % ns}, device_id_type=MESH
        )
    pl.semaphore_wait(barrier, bits + ns - 1)

    slots = [slot_of(f, order) for order in orders]
    for h in range(2):
        gathered[h, slots[h]] = weight_t[h * part_heads : (h + 1) * part_heads]
    for i in range(bits):
        copies = []
        for h in range(2):
            part = gathered.at[h, pl.ds((slots[h] // 2**i) * 2**i, 2**i)]
            copy = pltpu.make_async_remote_copy(
                src_ref=part,
                dst_ref=part,
                send_sem=ag_ssem.at[h, i],
                recv_sem=ag_rsem.at[h, i],
                device_id={"fsdp": partner(orders[h][i])},
                device_id_type=MESH,
            )
            copy.start()
            copies.append(copy)
        if i == bits - 1:
            for load in loads:
                load.wait()
        for copy in copies:
            copy.wait()

    raw = jnp.broadcast_to(bias[...], (length, heads)).T
    rate = jnp.broadcast_to(rate_row[...], (length, heads)).T
    for own in range(nf):
        weight = jnp.concatenate(
            [gathered[h, slot_of(own, orders[h])] for h in range(2)], axis=0
        )
        raw = raw + dot(weight, tokens[:, own * rows : (own + 1) * rows], 1, 1)
    step = jnp.maximum(raw, 0.0) + jnp.log1p(jnp.exp(-jnp.abs(raw)))
    before = iota((length, length), 0) <= iota((length, length), 1)
    cum = dot(-rate * step, before.astype(F32), precision=HIGH)
    raw_t[...] = raw
    cum_t[...] = cum
    step_t[...] = step
    final = cum[:, length - 1 : length]
    block_t[...] = jnp.broadcast_to(jnp.exp(final), (heads, STATE))
    both = jnp.concatenate([cum, step], axis=0).T
    cum_c = both[:, :heads]
    step_c = both[:, heads:]
    tail_c = jnp.exp(cum_c[length - 1 : length] - cum_c)
    lead_c = jnp.exp(cum_c)
    for g in range(groups):
        span = slice(g * per, (g + 1) * per)
        cum_g[g] = cum_c[:, span]
        step_g[g] = step_c[:, span]
        tail_g[g] = tail_c[:, span]
        lead_g[g] = lead_c[:, span]

    spread_one = (iota((2 * per, wide), 0) % per == iota((2 * per, wide), 1) // size).astype(BF16)
    gather_one = (iota((per, wide), 0) == iota((per, wide), 1) // size).astype(BF16)

    def expand(value):
        return dot(halves(value, 1), spread_one)

    def head_sums(value):
        high = value.astype(BF16)
        low = (value - high.astype(F32)).astype(BF16)
        return dot(gather_one, high, 1, 1) + dot(gather_one, low, 1, 1)

    def span_of(g, width):
        return pl.ds(pl.multiple_of(g * width, width), width)

    @pl.when(z == 0)
    def _():
        entry[...] = jnp.zeros_like(entry)

    @pl.when(z == ns - 1)
    def _():
        later[...] = jnp.zeros_like(later)

    spread_half = (
        iota((per, chunk), 0) % (per // 2) == iota((per, chunk), 1) // size
    ).astype(BF16)

    def piece(g):
        return g // 2, pl.ds(pl.multiple_of((g % 2) * chunk, chunk), chunk)

    def forward_copy(g):
        return pltpu.make_async_remote_copy(
            src_ref=send_f.at[piece(g)],
            dst_ref=entry.at[piece(g)],
            send_sem=f_ssem.at[g],
            recv_sem=f_rsem.at[g],
            device_id={"seq": (z + 1) % ns},
            device_id_type=MESH,
        )

    def backward_copy(g):
        return pltpu.make_async_remote_copy(
            src_ref=send_b.at[piece(g)],
            dst_ref=later.at[piece(g)],
            send_sem=b_ssem.at[g],
            recv_sem=b_rsem.at[g],
            device_id={"seq": (z + ns - 1) % ns},
            device_id_type=MESH,
        )

    def local(g):
        xs = (x[:, span_of(g, wide)].astype(F32) * expand(step_g[g] * tail_g[g])).astype(BF16)
        ds = (dy[:, span_of(g, wide)].astype(F32) * expand(lead_g[g])).astype(BF16)
        xs_g[g] = xs
        ds_g[g] = ds
        state_loc[g] = dot(xs, b_in[:, span_of(g, STATE)], 0, 0)
        grad_loc[g] = dot(ds, c_out[:, span_of(g, STATE)], 0, 0)

    def decay_rows(g):
        return dot(spread_half, halves(block_t[span_of(g, per // 2)], 0), 0, 0)

    def chain_f(g):
        @pl.when(z > 0)
        def _():
            forward_copy(g).wait_recv()

        @pl.when(z < ns - 1)
        def _():
            p = piece(g)
            send_f[p] = (decay_rows(g) * entry[p].astype(F32) + state_loc[p]).astype(BF16)
            forward_copy(g).start()

    def chain_b(g):
        @pl.when(z < ns - 1)
        def _():
            backward_copy(g).wait_recv()

        @pl.when(z > 0)
        def _():
            p = piece(g)
            send_b[p] = (decay_rows(g) * later[p].astype(F32) + grad_loc[p]).astype(BF16)
            backward_copy(g).start()

    def heavy(g):
        inputs = x[:, span_of(g, wide)]
        upstream = dy[:, span_of(g, wide)]
        b = b_in[:, span_of(g, STATE)]
        c = c_out[:, span_of(g, STATE)]
        meet = dot(b, c, 1, 1)
        upper = iota((length, length), 0) <= iota((length, length), 1)
        lanes = iota((length, 128), 1)
        cum_r = cum_t[span_of(g, per)]
        cum_l = cum_g[g]
        step_l = step_g[g]
        joint = jnp.zeros((length, length), F32)
        sums = []
        pieces = []
        for q in range(wide // 128):
            x_q = inputs[:, q * 128 : (q + 1) * 128]
            dy_q = upstream[:, q * 128 : (q + 1) * 128]
            weights = []
            masked = []
            for j in range(128 // size):
                k = q * (128 // size) + j
                mine = lanes // size == j
                pair = dot(jnp.where(mine, x_q, jnp.zeros_like(x_q)), dy_q, 1, 1)
                spread = cum_r[k : k + 1] - cum_l[:, k : k + 1]
                decay = jnp.exp(jnp.where(upper, spread, -1e30))
                weights.append((decay * meet).astype(BF16))
                masked.append(jnp.where(mine, dy_q, jnp.zeros_like(dy_q)))
                scaled = decay * pair * step_l[:, k : k + 1]
                joint = joint + scaled
                sums.append(jnp.sum(scaled * meet, axis=0, keepdims=True))
            pieces.append(
                dot(jnp.concatenate(weights, axis=1), jnp.concatenate(masked, axis=0))
            )
        passed = jnp.concatenate(pieces, axis=1)
        through[g] = passed
        col_t[span_of(g, per)] = jnp.concatenate(sums, axis=0)
        xt_t[span_of(g, per)] = head_sums(inputs.astype(F32) * passed)
        joint = joint.astype(BF16)
        grad_b[g] = dot(joint, c)
        grad_c[g] = dot(joint, b, 0, 0)

    def finish_f(g):
        c = c_out[:, span_of(g, STATE)]
        read = dot(c, entry[g], 1, 1)
        ent_t[span_of(g, per)] = head_sums(ds_g[g].astype(F32) * read)
        out_c[:, span_of(g, STATE)] = (grad_c[g] + dot(ds_g[g], entry[g])).astype(BF16)

    def finish_b(g):
        b = b_in[:, span_of(g, STATE)]
        carried = dot(b, later[g], 1, 1)
        xc_t[span_of(g, per)] = head_sums(x[:, span_of(g, wide)].astype(F32) * carried)
        inner = through[g] + expand(tail_g[g]) * carried
        out_x[:, span_of(g, wide)] = (expand(step_g[g]) * inner).astype(BF16)
        out_b[:, span_of(g, STATE)] = (grad_b[g] + dot(xs_g[g], later[g])).astype(BF16)

    def within(g):
        return jnp.logical_and(g >= 0, g < groups)

    def slot_step(tau, carry):
        gf = tau - z
        gb = tau - (ns - 1 - z)
        pl.when(tau < groups)(lambda: local(tau))
        pl.when(within(gf))(lambda: chain_f(2 * gf))
        pl.when(within(gb))(lambda: chain_b(2 * gb))
        pl.when(tau < groups)(lambda: heavy(tau))
        pl.when(within(gf))(lambda: chain_f(2 * gf + 1))
        pl.when(within(gb))(lambda: chain_b(2 * gb + 1))
        pl.when(within(gf))(lambda: finish_f(gf))
        pl.when(within(gb))(lambda: finish_b(gb))
        return carry

    lax.fori_loop(0, groups + ns - 1, slot_step, 0)
    stores = [
        pltpu.make_async_copy(source, target, out_sem.at[n])
        for n, (source, target) in enumerate(
            ((out_x, x_out), (out_b, b_out), (out_c, c_out_hbm))
        )
    ]
    for store in stores:
        store.start()

    crossing = jnp.concatenate(
        [
            dot(gather_one, (entry[g].astype(F32) * later[g].astype(F32)).astype(BF16))
            for g in range(groups)
        ],
        axis=0,
    )
    cum = cum_t[...]
    step = step_t[...]
    raw = raw_t[...]
    tail = jnp.exp(cum[:, length - 1 : length] - cum)
    xt = xt_t[...]
    tail_xc = tail * xc_t[...]
    leaving = step * tail_xc
    grad_cum = col_t[...] - step * xt + ent_t[...] - leaving
    closing = block_t[:, :1] * jnp.sum(crossing, axis=1, keepdims=True) + jnp.sum(
        leaving, axis=1, keepdims=True
    )
    after = (iota((length, length), 0) >= iota((length, length), 1)).astype(F32)
    grad_log = dot(grad_cum, after, precision=HIGH) + closing
    grad_raw = (xt + tail_xc - rate * grad_log) * jax.nn.sigmoid(raw)
    grad_raw = grad_raw.astype(BF16)

    bases = [0, 0]
    count = nf
    early = rows % 128 == 0

    def product(own, target, place, offset):
        columns = pl.ds(pl.multiple_of(own * rows, 128), rows) if early else slice(
            own * rows, (own + 1) * rows
        )
        block = dot(grad_raw, tokens[:, columns])
        for h in range(2):
            target[h, offset + place[h]] = block[
                h * part_heads : (h + 1) * part_heads
            ].astype(target.dtype)

    for j in range(bits):
        half = count // 2
        sent = pl.ds(nf - count, half)
        if j == 0 and early:
            bit = f % 2
            for i in range(half):
                place = [slot_of(2 * i, order) for order in orders]
                product(2 * i + (1 - bit), rs_send, place, 0)
        elif j == 0:
            for own in range(nf):
                product(own, total, [slot_of(own, order) for order in orders], 0)
        copies = []
        for h in range(2):
            b = orders[h][bits - 1 - j]
            bit_h = (f // 2**b) % 2
            if j > 0 or not early:
                rs_send[h, sent] = total[
                    h, pl.ds(bases[h] + (1 - bit_h) * half, half)
                ].astype(BF16)
            copy = pltpu.make_async_remote_copy(
                src_ref=rs_send.at[h, sent],
                dst_ref=rs_recv.at[h, sent],
                send_sem=rs_ssem.at[h, j],
                recv_sem=rs_rsem.at[h, j],
                device_id={"fsdp": partner(b)},
                device_id_type=MESH,
            )
            copy.start()
            copies.append(copy)
            bases[h] = bases[h] + bit_h * half
        if j == 0 and early:
            for i in range(half):
                place = [slot_of(2 * i, order) for order in orders]
                product(2 * i + bit, total, place, bit * half)
        for h in range(2):
            copies[h].wait()
            total[h, pl.ds(bases[h], half)] += rs_recv[h, sent].astype(F32)
        count = half

    z_recv[z] = jnp.concatenate([total[h, bases[h]] for h in range(2)], axis=0).astype(BF16)
    copies = []
    for d in range(1, ns):
        copy = pltpu.make_async_remote_copy(
            src_ref=z_recv.at[z],
            dst_ref=z_recv.at[z],
            send_sem=z_ssem.at[d - 1],
            recv_sem=z_rsem.at[d - 1],
            device_id={"seq": (z + d) % ns},
            device_id_type=MESH,
        )
        copy.start()
        copies.append(copy)
    for copy in copies:
        copy.wait()
    summed = z_recv[0].astype(F32)
    for k in range(1, ns):
        summed = summed + z_recv[k].astype(F32)
    out_w[...] = summed

    @pl.when(z < ns - 1)
    def _():
        for g in range(2 * groups):
            forward_copy(g).wait_send()

    @pl.when(z > 0)
    def _():
        for g in range(2 * groups):
            backward_copy(g).wait_send()

    for store in stores:
        store.wait()


def body(
    layer_input, dt_weight, dt_bias, decay_rate, ssm_input, in_basis, out_basis, out_cotangent
):
    nf, ns = lax.axis_size("fsdp"), lax.axis_size("seq")
    length = layer_input.shape[1]
    rows, heads = dt_weight.shape
    groups = in_basis.shape[2] // STATE
    per = heads // groups
    full = ssm_input.shape[2]
    wide = full // groups
    bits = nf.bit_length() - 1
    tall = (groups, wide, STATE)
    dma = pltpu.SemaphoreType.DMA
    v = pltpu.VMEM
    scratch = [
        v((length, layer_input.shape[2]), BF16),
        v((length, full), BF16),
        v((length, groups * STATE), BF16),
        v((length, groups * STATE), BF16),
        v((length, full), BF16),
        v((length, full), BF16),
        v((length, groups * STATE), BF16),
        v((length, groups * STATE), BF16),
        dma((5,)),
        dma((3,)),
        v((2, nf, heads // 2, rows), BF16),
        v((heads, length), F32),
        v((heads, length), F32),
        v((heads, length), F32),
        v((heads, STATE), F32),
        v((groups, length, per), F32),
        v((groups, length, per), F32),
        v((groups, length, per), F32),
        v((groups, length, per), F32),
        v(tall, F32),
        v(tall, F32),
        v((groups, length, wide), BF16),
        v((groups, length, wide), BF16),
        v(tall, BF16),
        v(tall, BF16),
        v(tall, BF16),
        v(tall, BF16),
        v((groups, length, wide), F32),
        v((groups, length, STATE), F32),
        v((groups, length, STATE), F32),
        v((heads, length), F32),
        v((heads, length), F32),
        v((heads, length), F32),
        v((heads, length), F32),
        v((2, nf, heads // 2, rows), F32),
        v((2, nf, heads // 2, rows), BF16),
        v((2, nf, heads // 2, rows), BF16),
        v((ns, heads, rows), BF16),
        dma((2, bits)),
        dma((2, bits)),
        dma((2 * groups,)),
        dma((2 * groups,)),
        dma((2 * groups,)),
        dma((2 * groups,)),
        dma((2, bits)),
        dma((2, bits)),
        dma((ns - 1,)),
        dma((ns - 1,)),
    ]
    anywhere = pl.BlockSpec(memory_space=pl.ANY)
    inside = pl.BlockSpec(memory_space=pltpu.VMEM)
    out_x, out_b, out_c, out_w = pl.pallas_call(
        functools.partial(kernel, nf, ns),
        out_shape=(
            jax.ShapeDtypeStruct((length, full), BF16),
            jax.ShapeDtypeStruct((length, groups * STATE), BF16),
            jax.ShapeDtypeStruct((length, groups * STATE), BF16),
            jax.ShapeDtypeStruct((heads, rows), F32),
        ),
        in_specs=[anywhere] + [inside] * 3 + [anywhere] * 4,
        out_specs=[anywhere] * 3 + [inside],
        scratch_shapes=scratch,
        compiler_params=pltpu.CompilerParams(
            collective_id=0, has_side_effects=True, vmem_limit_bytes=60 * 1024 * 1024
        ),
    )(
        layer_input[0],
        dt_weight.T,
        dt_bias[None],
        decay_rate[None],
        ssm_input[0],
        in_basis[0],
        out_basis[0],
        out_cotangent[0],
    )
    return (out_x[None], out_b[None], out_c[None], out_w.T)


def solution(mesh):
    blocks = P("fsdp", "seq", None)
    rows = P("fsdp", None)
    return jax.shard_map(
        body,
        mesh=mesh,
        in_specs=(blocks, rows, P(), P(), blocks, blocks, blocks, blocks),
        out_specs=(blocks, blocks, blocks, rows),
        check_vma=False,
    )
```

profile of v0, /device:TPU:0, one launch (start us, length us, event | category | flops | bytes accessed | tf_op | source)
XLA Modules:
  0.0 59.2 jit_solution(11027189856904310001)
XLA Ops:
  0.6 54.1 %shard_map.111 = (bf16[128,2048]{1,0:T(8,128)(2,1)}, bf16[128,512]{1,0:T(8,128)(2,1)}, bf16[128,512]{1,0:T(8,128)(2,1)}, f32[64,512]{1,0:T(8,128)}) custom-call(bf16[128,4096]{1,0:T(8,128)(2,1)} %bitcast.12, bf16[64,512]{1,0:T(8,128)(2,1)} %bitcast.21, f32[1,64]{1,0:T(1,128)} %bitcast.22, f32[1,64]{1,0:T(1,128)} %bitcast.23, bf16[128,2048]{1,0:T(8,128)(2,1)} %bitcast.14, ...), custom_call_target="tpu_custom_call" | custom-call | tf_op jit(solution)/shard_map/pallas_call | solution.py:530
  54.7 0.0 copy-start.2
  54.7 1.9 %copy.16 = bf16[1,128,2048]{2,1,0:T(8,128)(2,1)} copy(bf16[1,128,2048]{2,1,0:T(8,128)(2,1)} %bitcast.13) | data formatting | bytes 1048576
  56.7 0.0 copy-done.2
  56.7 0.0 copy-start.1
  56.7 0.7 %copy.17 = bf16[1,128,512]{2,1,0:T(8,128)(2,1)} copy(bf16[1,128,512]{2,1,0:T(8,128)(2,1)S(1)} %bitcast.20) | data formatting | bytes 262144
  57.3 0.3 copy-done.1
  57.6 0.0 copy-start
  57.6 0.7 %copy.18 = bf16[1,128,512]{2,1,0:T(8,128)(2,1)} copy(bf16[1,128,512]{2,1,0:T(8,128)(2,1)S(1)} %bitcast.19) | data formatting | bytes 262144
  58.3 0.3 copy-done
  58.6 0.7 %copy.19 = f32[512,64]{0,1:T(8,128)} copy(f32[512,64]{0,1:T(8,128)S(1)} %bitcast.18) | data formatting | bytes 262144
Async XLA Ops:
  54.7 1.9 %copy-start.2 = (bf16[128,512]{1,0:T(8,128)(2,1)S(1)}, bf16[128,512]{1,0:T(8,128)(2,1)}, u32[]{:S(2)}) copy-start(bf16[128,512]{1,0:T(8,128)(2,1)} %get-tuple-element.9) | copy-start | bytes 393220
  56.7 1.0 %copy-start.1 = (bf16[128,512]{1,0:T(8,128)(2,1)S(1)}, bf16[128,512]{1,0:T(8,128)(2,1)}, u32[]{:S(2)}) copy-start(bf16[128,512]{1,0:T(8,128)(2,1)} %get-tuple-element.10) | copy-start | bytes 393220
  57.6 1.0 %copy-start = (f32[64,512]{1,0:T(8,128)S(1)}, f32[64,512]{1,0:T(8,128)}, u32[]{:S(2)}) copy-start(f32[64,512]{1,0:T(8,128)} %get-tuple-element.11) | copy-start | bytes 393220
where the time goes:
time: 59.4 us; the launch traced here: 59.2 us
  Pallas kernels  54.1 us (91%)
  local copies, waits for them, and re-layouts  4.48 us (8%)
  between operations  0.65 us (1%)
    pallas_call x1, Pallas kernels, body(): pl.pallas_call(functools.partial(kernel, nf, ns), out_shape=(jax.ShapeDty...  54.1 us
    unnamed x10, local copies, waits for them, and re-layouts  4.48 us

commit v1 on v0

--- a/solution.py
+++ b/solution.py
@@ -30,7 +30,505 @@
     return lax.broadcasted_iota(jnp.int32, shape, dim)
 
 
+QUARTER = 128
+
+
 def kernel(
+    nf,
+    ns,
+    tokens_hbm,
+    weight_hbm,
+    bias_hbm,
+    rate_hbm,
+    x_hbm,
+    b_hbm,
+    c_hbm,
+    dy_hbm,
+    out_x,
+    out_b,
+    out_c,
+    out_w,
+    tokens,
+    bias,
+    rate_row,
+    x,
+    b_in,
+    c_out,
+    dy,
+    in_sem,
+    own_sem,
+    gathered,
+    gathered_x,
+    gathered_r,
+    bias_t,
+    rate_t,
+    raw_t,
+    cum_t,
+    step_t,
+    block_t,
+    cum_g,
+    step_g,
+    decay_g,
+    meet_g,
+    spread_s,
+    spread_st,
+    state_loc,
+    grad_loc,
+    xs_g,
+    ds_g,
+    entry,
+    later,
+    send_f,
+    send_b,
+    through,
+    joint,
+    grad_b,
+    grad_c,
+    acc_b,
+    acc_c,
+    col_t,
+    xt_t,
+    xc_t,
+    ent_t,
+    z_early,
+    z_last,
+    ag_ssem,
+    ag_rsem,
+    x_ssem,
+    x_rsem,
+    r_ssem,
+    r_rsem,
+    f_ssem,
+    f_rsem,
+    b_ssem,
+    b_rsem,
+    z_ssem,
+    z_rsem,
+):
+    f = lax.axis_index("fsdp")
+    z = lax.axis_index("seq")
+    length = tokens.shape[0]
+    heads, rows = weight_hbm.shape
+    groups = b_in.shape[1] // STATE
+    per = heads // groups
+    wide = x.shape[1] // groups
+    size = wide // per
+    quarters = wide // QUARTER
+    few = QUARTER // size
+    bits = nf.bit_length() - 1
+    last = groups - 1
+
+    def partner(m):
+        return f + sum(
+            (1 - 2 * ((f // 2**j) % 2)) * 2**j for j in range(bits) if (m // 2**j) % 2
+        )
+
+    far_first = sorted(range(1, nf), key=lambda m: -bin(m // 2).count("1"))
+
+    own_weight = pltpu.make_async_copy(weight_hbm, gathered.at[f], own_sem.at[0])
+    own_weight.start()
+    barrier = pltpu.get_barrier_semaphore()
+    for m in far_first:
+        pl.semaphore_signal(
+            barrier, inc=1, device_id={"fsdp": partner(m)}, device_id_type=MESH
+        )
+
+    @pl.when(z < ns - 1)
+    def _():
+        pl.semaphore_signal(
+            barrier, inc=1, device_id={"seq": z + 1}, device_id_type=MESH
+        )
+
+    @pl.when(z > 0)
+    def _():
+        pl.semaphore_signal(
+            barrier, inc=1, device_id={"seq": z - 1}, device_id_type=MESH
+        )
+
+    loads = [
+        pltpu.make_async_copy(source, target, in_sem.at[n])
+        for n, (source, target) in enumerate(
+            (
+                (bias_hbm, bias),
+                (rate_hbm, rate_row),
+                (tokens_hbm, tokens),
+                (x_hbm, x),
+                (b_hbm, b_in),
+                (dy_hbm, dy),
+                (c_hbm, c_out),
+            )
+        )
+    ]
+    for load in loads:
+        load.start()
+    loads[0].wait()
+    loads[1].wait()
+    bias_t[...] = jnp.broadcast_to(bias[...], (length, heads)).T
+    rate_t[...] = jnp.broadcast_to(rate_row[...], (length, heads)).T
+    own_weight.wait()
+    ends = (z > 0).astype(jnp.int32) + (z < ns - 1).astype(jnp.int32)
+    pl.semaphore_wait(barrier, nf - 1 + ends)
+
+    def span_of(g, width):
+        start = g * width
+        return pl.ds(start if isinstance(start, int) else pl.multiple_of(start, width), width)
+
+    def weight_copy(g, m):
+        part = gathered.at[f, span_of(g, per)]
+        return pltpu.make_async_remote_copy(
+            src_ref=part,
+            dst_ref=part,
+            send_sem=ag_ssem.at[g, m - 1],
+            recv_sem=ag_rsem.at[g, m - 1],
+            device_id={"fsdp": partner(m)},
+            device_id_type=MESH,
+        )
+
+    def token_copy(m):
+        return pltpu.make_async_remote_copy(
+            src_ref=tokens.at[:, span_of(partner(m), rows)],
+            dst_ref=gathered_x.at[span_of(f, length)],
+            send_sem=x_ssem.at[m - 1],
+            recv_sem=x_rsem.at[m - 1],
+            device_id={"fsdp": partner(m)},
+            device_id_type=MESH,
+        )
+
+    def raw_copy(g, m):
+        part = gathered_r.at[f, span_of(g, per)]
+        return pltpu.make_async_remote_copy(
+            src_ref=part,
+            dst_ref=part,
+            send_sem=r_ssem.at[g, m - 1],
+            recv_sem=r_rsem.at[g, m - 1],
+            device_id={"fsdp": partner(m)},
+            device_id_type=MESH,
+        )
+
+    for g in range(groups):
+        for m in far_first:
+            weight_copy(g, m).start()
+    for load in loads[2:]:
+        load.wait()
+    own_tokens = pltpu.make_async_copy(
+        tokens.at[:, span_of(f, rows)], gathered_x.at[span_of(f, length)], own_sem.at[1]
+    )
+    own_tokens.start()
+    for m in far_first:
+        token_copy(m).start()
+
+    @pl.when(z == 0)
+    def _():
+        entry[...] = jnp.zeros_like(entry)
+
+    @pl.when(z == ns - 1)
+    def _():
+        later[...] = jnp.zeros_like(later)
+
+    spread_one = (iota((2 * per, wide), 0) % per == iota((2 * per, wide), 1) // size).astype(BF16)
+    gather_one = (iota((per, wide), 0) == iota((per, wide), 1) // size).astype(BF16)
+
+    def expand(value):
+        return dot(halves(value, 1), spread_one)
+
+    def head_sums(value):
+        width = value.shape[1]
+        ones = (iota((width // size, width), 0) == iota((width // size, width), 1) // size).astype(BF16)
+        high = value.astype(BF16)
+        low = (value - high.astype(F32)).astype(BF16)
+        return dot(ones, high, 1, 1) + dot(ones, low, 1, 1)
+
+    def strip(q, n=1):
+        return slice(q * QUARTER, (q + n) * QUARTER)
+
+    def forward_copy(g, q):
+        return pltpu.make_async_remote_copy(
+            src_ref=send_f.at[g, strip(q)],
+            dst_ref=entry.at[g, strip(q)],
+            send_sem=f_ssem.at[g, q],
+            recv_sem=f_rsem.at[g, q],
+            device_id={"seq": (z + 1) % ns},
+            device_id_type=MESH,
+        )
+
+    def backward_copy(g, q):
+        return pltpu.make_async_remote_copy(
+            src_ref=send_b.at[g, strip(q)],
+            dst_ref=later.at[g, strip(q)],
+            send_sem=b_ssem.at[g, q],
+            recv_sem=b_rsem.at[g, q],
+            device_id={"seq": (z + ns - 1) % ns},
+            device_id_type=MESH,
+        )
+
+    def prepare(g):
+        for m in range(1, nf):
+            weight_copy(g, m).wait_recv()
+        mine = span_of(g, per)
+        weight = jnp.concatenate([gathered[own, mine] for own in range(nf)], axis=1)
+        rate = rate_t[mine]
+        raw = bias_t[mine] + dot(weight, tokens[...], 1, 1)
+        step = jnp.maximum(raw, 0.0) + jnp.log1p(jnp.exp(-jnp.abs(raw)))
+        before = iota((length, length), 0) <= iota((length, length), 1)
+        cum = dot(-rate * step, before.astype(F32), precision=HIGH)
+        raw_t[mine] = raw
+        cum_t[mine] = cum
+        step_t[mine] = step
+        final = cum[:, length - 1 : length]
+        block = jnp.broadcast_to(jnp.exp(final), (per, STATE))
+        block_t[mine] = block
+        decay_g[g] = dot(spread_one, halves(block, 0), 0, 0)
+        both = jnp.concatenate([cum, step], axis=0).T
+        cum_c = both[:, :per]
+        step_c = both[:, per:]
+        cum_g[g] = cum_c
+        step_g[g] = step_c
+        scale = expand(step_c * jnp.exp(cum_c[length - 1 : length] - cum_c))
+        spread_st[g] = scale
+        b = b_in[:, span_of(g, STATE)]
+        c = c_out[:, span_of(g, STATE)]
+        xs = (x[:, span_of(g, wide)].astype(F32) * scale).astype(BF16)
+        ds = (dy[:, span_of(g, wide)].astype(F32) * expand(jnp.exp(cum_c))).astype(BF16)
+        xs_g[g] = xs
+        ds_g[g] = ds
+        state = dot(xs, b, 0, 0)
+        grad = dot(ds, c, 0, 0)
+        state_loc[g] = state
+        grad_loc[g] = grad
+
+        @pl.when(z == 0)
+        def _():
+            send_f[g] = state.astype(BF16)
+            for q in range(quarters):
+                forward_copy(g, q).start()
+
+        @pl.when(z == ns - 1)
+        def _():
+            send_b[g] = grad.astype(BF16)
+            for q in range(quarters):
+                backward_copy(g, q).start()
+
+        spread_s[g] = expand(step_c)
+        meet_g[g] = dot(b, c, 1, 1)
+
+    def chain_f(g, q):
+        @pl.when(z > 0)
+        def _():
+            forward_copy(g, q).wait_recv()
+
+        @pl.when(jnp.logical_and(z > 0, z < ns - 1))
+        def _():
+            s = strip(q)
+            send_f[g, s] = (decay_g[g, s] * entry[g, s].astype(F32) + state_loc[g, s]).astype(BF16)
+            forward_copy(g, q).start()
+
+    def chain_b(g, q):
+        @pl.when(z < ns - 1)
+        def _():
+            backward_copy(g, q).wait_recv()
+
+        @pl.when(jnp.logical_and(z > 0, z < ns - 1))
+        def _():
+            s = strip(q)
+            send_b[g, s] = (decay_g[g, s] * later[g, s].astype(F32) + grad_loc[g, s]).astype(BF16)
+            backward_copy(g, q).start()
+
+    def columns(g, q, n=1):
+        return pl.ds(pl.multiple_of(g * wide + q * QUARTER, QUARTER), n * QUARTER)
+
+    def heavy(g, q):
+        x_q = x[:, columns(g, q)]
+        dy_q = dy[:, columns(g, q)]
+        meet = meet_g[g]
+        upper = iota((length, length), 0) <= iota((length, length), 1)
+        lanes = iota((length, QUARTER), 1)
+        cum_r = cum_t[span_of(g, per)]
+        cum_l = cum_g[g]
+        step_l = step_g[g]
+        total = jnp.zeros((length, length), F32) if q == 0 else joint[...]
+        sums = []
+        weights = []
+        masked = []
+        for j in range(few):
+            k = q * few + j
+            mine = lanes // size == j
+            pair = dot(jnp.where(mine, x_q, jnp.zeros_like(x_q)), dy_q, 1, 1)
+            spread = cum_r[k : k + 1] - cum_l[:, k : k + 1]
+            decay = jnp.exp(jnp.where(upper, spread, -1e30))
+            weights.append((decay * meet).astype(BF16))
+            masked.append(jnp.where(mine, dy_q, jnp.zeros_like(dy_q)))
+            scaled = decay * pair * step_l[:, k : k + 1]
+            total = total + scaled
+            sums.append(jnp.sum(scaled * meet, axis=0, keepdims=True))
+        passed = dot(jnp.concatenate(weights, axis=1), jnp.concatenate(masked, axis=0))
+        through[g, :, strip(q)] = spread_s[g, :, strip(q)] * passed
+        col_t[g, q] = jnp.concatenate(sums, axis=0)
+        xt_t[g, q] = head_sums(x_q.astype(F32) * passed)
+        if q < quarters - 1:
+            joint[...] = total
+        else:
+            total = total.astype(BF16)
+            grad_b[g] = dot(total, c_out[:, span_of(g, STATE)])
+            grad_c[g] = dot(total, b_in[:, span_of(g, STATE)], 0, 0)
+
+    def finish_f(g, q, n):
+        c = c_out[:, span_of(g, STATE)]
+        state = entry[g, strip(q, n)]
+        ds = ds_g[g, :, strip(q, n)]
+        sums = head_sums(ds.astype(F32) * dot(c, state, 1, 1))
+        for i in range(n):
+            ent_t[g, q + i] = sums[i * few : (i + 1) * few]
+        value = dot(ds, state)
+        if q > 0:
+            value = value + acc_c[...]
+        if q + n < quarters:
+            acc_c[...] = value
+        else:
+            out_c[:, span_of(g, STATE)] = (grad_c[g] + value).astype(BF16)
+
+    def finish_b(g, q, n):
+        b = b_in[:, span_of(g, STATE)]
+        grad = later[g, strip(q, n)]
+        carried = dot(b, grad, 1, 1)
+        sums = head_sums(x[:, columns(g, q, n)].astype(F32) * carried)
+        for i in range(n):
+            xc_t[g, q + i] = sums[i * few : (i + 1) * few]
+        out_x[:, columns(g, q, n)] = (
+            through[g, :, strip(q, n)] + spread_st[g, :, strip(q, n)] * carried
+        ).astype(BF16)
+        value = dot(xs_g[g, :, strip(q, n)], grad)
+        if q > 0:
+            value = value + acc_b[...]
+        if q + n < quarters:
+            acc_b[...] = value
+        else:
+            out_b[:, span_of(g, STATE)] = (grad_b[g] + value).astype(BF16)
+
+    def post(g):
+        mine = span_of(g, per)
+        crossing = dot(
+            gather_one, (entry[g].astype(F32) * later[g].astype(F32)).astype(BF16)
+        )
+        cum = cum_t[mine]
+        step = step_t[mine]
+        rate = rate_t[mine]
+
+        def stacked(parts):
+            return jnp.concatenate([parts[g, q] for q in range(quarters)], axis=0)
+
+        xt = stacked(xt_t)
+        tail_xc = jnp.exp(cum[:, length - 1 : length] - cum) * stacked(xc_t)
+        leaving = step * tail_xc
+        grad_cum = stacked(col_t) - step * xt + stacked(ent_t) - leaving
+        closing = block_t[mine, :1] * jnp.sum(crossing, axis=1, keepdims=True) + jnp.sum(
+            leaving, axis=1, keepdims=True
+        )
+        after = (iota((length, length), 0) >= iota((length, length), 1)).astype(F32)
+        grad_log = dot(grad_cum, after, precision=HIGH) + closing
+        grad_raw = (xt + tail_xc - rate * grad_log) * jax.nn.sigmoid(raw_t[mine])
+        gathered_r[f, mine] = grad_raw.astype(BF16)
+        for m in far_first:
+            raw_copy(g, m).start()
+
+    def within(g):
+        return jnp.logical_and(g >= 0, g < groups)
+
+    furthest = jnp.maximum(z, ns - 1 - z)
+
+    def slot_step(tau, carry):
+        gf = tau - z
+        gb = tau - (ns - 1 - z)
+        for q in range(quarters):
+            pl.when(within(gf))(lambda: chain_f(gf, q))
+            pl.when(within(gb))(lambda: chain_b(gb, q))
+            if q == 0:
+                pl.when(tau + 1 < groups)(lambda: prepare(tau + 1))
+            pl.when(within(tau))(lambda: heavy(tau, q))
+            if (q + 1) % FINISH == 0:
+                at = q + 1 - FINISH
+                pl.when(within(gf))(lambda: finish_f(gf, at, FINISH))
+                pl.when(within(gb))(lambda: finish_b(gb, at, FINISH))
+        pl.when(within(tau - furthest))(lambda: post(tau - furthest))
+        return carry
+
+    lax.fori_loop(-1, groups + ns - 1, slot_step, 0)
+
+    def product(first, count):
+        raws = jnp.concatenate(
+            [gathered_r[own, first * per : (first + count) * per] for own in range(nf)], axis=1
+        )
+        return dot(raws, gathered_x[...]).astype(BF16)
+
+    def exchange(target, n):
+        copies = []
+        for d in range(1, ns):
+            copy = pltpu.make_async_remote_copy(
+                src_ref=target.at[z],
+                dst_ref=target.at[z],
+                send_sem=z_ssem.at[n, d - 1],
+                recv_sem=z_rsem.at[n, d - 1],
+                device_id={"seq": (z + d) % ns},
+                device_id_type=MESH,
+            )
+            copy.start()
+            copies.append(copy)
+        return copies
+
+    own_tokens.wait()
+    for m in range(1, nf):
+        token_copy(m).wait_recv()
+    for g in range(last):
+        for m in range(1, nf):
+            raw_copy(g, m).wait_recv()
+    z_early[z] = product(0, last)
+    early = exchange(z_early, 0)
+    for m in range(1, nf):
+        raw_copy(last, m).wait_recv()
+    z_last[z] = product(last, 1)
+    late = exchange(z_last, 1)
+    for copies, source, place in (
+        (early, z_early, slice(0, last * per)),
+        (late, z_last, slice(last * per, heads)),
+    ):
+        for copy in copies:
+            copy.wait()
+        summed = source[0].astype(F32)
+        for k in range(1, ns):
+            summed = summed + source[k].astype(F32)
+        out_w[place] = summed
+
+    for m in range(1, nf):
+        token_copy(m).wait_send()
+        for g in range(groups):
+            weight_copy(g, m).wait_send()
+            raw_copy(g, m).wait_send()
+
+    @pl.when(z < ns - 1)
+    def _():
+        for g in range(groups):
+            for q in range(quarters):
+                forward_copy(g, q).wait_send()
+
+    @pl.when(z > 0)
+    def _():
+        for g in range(groups):
+            for q in range(quarters):
+                backward_copy(g, q).wait_send()
+
+
+def ship(*refs):
+    sems = refs[-1]
+    count = len(refs) // 2
+    copies = [
+        pltpu.make_async_copy(refs[n], refs[count + n], sems.at[n]) for n in range(count)
+    ]
+    for copy in copies:
+        copy.start()
+    for copy in copies:
+        copy.wait()
+
+
+def general_kernel(
     nf,
     ns,
     tokens_hbm,
@@ -461,7 +959,7 @@
         store.wait()
 
 
-def body(
+def general_body(
     layer_input, dt_weight, dt_bias, decay_rate, ssm_input, in_basis, out_basis, out_cotangent
 ):
     nf, ns = lax.axis_size("fsdp"), lax.axis_size("seq")
@@ -528,7 +1026,7 @@
     anywhere = pl.BlockSpec(memory_space=pl.ANY)
     inside = pl.BlockSpec(memory_space=pltpu.VMEM)
     out_x, out_b, out_c, out_w = pl.pallas_call(
-        functools.partial(kernel, nf, ns),
+        functools.partial(general_kernel, nf, ns),
         out_shape=(
             jax.ShapeDtypeStruct((length, full), BF16),
             jax.ShapeDtypeStruct((length, groups * STATE), BF16),
@@ -554,11 +1052,136 @@
     return (out_x[None], out_b[None], out_c[None], out_w.T)
 
 
+FINISH = 2
+
+
+def body(
+    layer_input, dt_weight, dt_bias, decay_rate, ssm_input, in_basis, out_basis, out_cotangent
+):
+    nf, ns = lax.axis_size("fsdp"), lax.axis_size("seq")
+    length = layer_input.shape[1]
+    rows, heads = dt_weight.shape
+    groups = in_basis.shape[2] // STATE
+    per = heads // groups
+    full = ssm_input.shape[2]
+    wide = full // groups
+    size = wide // per
+    quarters = wide // QUARTER
+    few = QUARTER // size
+    tall = (groups, wide, STATE)
+    flat = (groups, length, wide)
+    dma = pltpu.SemaphoreType.DMA
+    v = pltpu.VMEM
+    scratch = [
+        v((length, layer_input.shape[2]), BF16),
+        v((1, heads), F32),
+        v((1, heads), F32),
+        v((length, full), BF16),
+        v((length, groups * STATE), BF16),
+        v((length, groups * STATE), BF16),
+        v((length, full), BF16),
+        dma((7,)),
+        dma((2,)),
+        v((nf, heads, rows), BF16),
+        v((nf * length, rows), BF16),
+        v((nf, heads, length), BF16),
+        v((heads, length), F32),
+        v((heads, length), F32),
+        v((heads, length), F32),
+        v((heads, length), F32),
+        v((heads, length), F32),
+        v((heads, STATE), F32),
+        v((groups, length, per), F32),
+        v((groups, length, per), F32),
+        v(tall, F32),
+        v((groups, length, length), F32),
+        v(flat, F32),
+        v(flat, F32),
+        v(tall, F32),
+        v(tall, F32),
+        v(flat, BF16),
+        v(flat, BF16),
+        v(tall, BF16),
+        v(tall, BF16),
+        v(tall, BF16),
+        v(tall, BF16),
+        v(flat, F32),
+        v((length, length), F32),
+        v((groups, length, STATE), F32),
+        v((groups, length, STATE), F32),
+        v((length, STATE), F32),
+        v((length, STATE), F32),
+        v((groups, quarters, few, length), F32),
+        v((groups, quarters, few, length), F32),
+        v((groups, quarters, few, length), F32),
+        v((groups, quarters, few, length), F32),
+        v((ns, heads - per, rows), BF16),
+        v((ns, per, rows), BF16),
+        dma((groups, nf - 1)),
+        dma((groups, nf - 1)),
+        dma((nf - 1,)),
+        dma((nf - 1,)),
+        dma((groups, nf - 1)),
+        dma((groups, nf - 1)),
+        dma((groups, quarters)),
+        dma((groups, quarters)),
+        dma((groups, quarters)),
+        dma((groups, quarters)),
+        dma((2, ns - 1)),
+        dma((2, ns - 1)),
+    ]
+    inside = pl.BlockSpec(memory_space=pltpu.VMEM)
+    outside = pl.BlockSpec(memory_space=pltpu.HBM)
+    operands = (
+        layer_input[0],
+        dt_weight.T,
+        dt_bias[None],
+        decay_rate[None],
+        ssm_input[0],
+        in_basis[0],
+        out_basis[0],
+        out_cotangent[0],
+    )
+    results = pl.pallas_call(
+        functools.partial(kernel, nf, ns),
+        out_shape=(
+            jax.ShapeDtypeStruct((length, full), BF16),
+            jax.ShapeDtypeStruct((length, groups * STATE), BF16),
+            jax.ShapeDtypeStruct((length, groups * STATE), BF16),
+            jax.ShapeDtypeStruct((heads, rows), F32),
+        ),
+        in_specs=[outside] * len(operands),
+        out_specs=[inside] * 4,
+        scratch_shapes=scratch,
+        compiler_params=pltpu.CompilerParams(
+            collective_id=0, has_side_effects=True, vmem_limit_bytes=40 * 1024 * 1024
+        ),
+    )(*[pltpu.with_memory_space_constraint(a, pltpu.HBM) for a in operands])
+    anywhere = pl.BlockSpec(memory_space=pl.ANY)
+    out_x, out_b, out_c, out_w = pl.pallas_call(
+        ship,
+        out_shape=[jax.ShapeDtypeStruct(r.shape, r.dtype) for r in results],
+        in_specs=[anywhere] * 4,
+        out_specs=[anywhere] * 4,
+        scratch_shapes=[dma((4,))],
+        compiler_params=pltpu.CompilerParams(vmem_limit_bytes=1024 * 1024),
+    )(*results)
+    return (out_x[None], out_b[None], out_c[None], out_w.T)
+
+
 def solution(mesh):
     blocks = P("fsdp", "seq", None)
     rows = P("fsdp", None)
+
+    def local(*args):
+        nf = lax.axis_size("fsdp")
+        shard = args[1].shape[0]
+        lanes = args[4].shape[2] * STATE // args[5].shape[2]
+        fits = shard % 128 == 0 and nf & (nf - 1) == 0 and lanes % QUARTER == 0
+        return (body if fits else general_body)(*args)
+
     return jax.shard_map(
-        body,
+        local,
         mesh=mesh,
         in_specs=(blocks, rows, P(), P(), blocks, blocks, blocks, blocks),
         out_specs=(blocks, blocks, blocks, rows),

time: 59.4 us -> 46.8 us (0.79)
  Pallas kernels: 54.1 us -> 46 us
  local copies, waits for them, and re-layouts: 4.48 us -> 0 us
    pallas_call x1, Pallas kernels: 54.1 us -> 45.1 us  [body(): pl.pallas_call(functools.partial(kernel, nf, ns), out_shape=(jax.ShapeDty...]
    unnamed x10 -> x0, local copies, waits for them, and re-layouts: 4.48 us -> none
    pallas_call x0 -> x1, Pallas kernels: none -> 0.95 us  [body(): pl.pallas_call(ship, out_shape=[jax.ShapeDtypeStruct(r.shape, r.dtype) fo...]
where the time goes in v1:
time: 46.8 us; the launch traced here: 46.7 us
  Pallas kernels  46 us (98%)
  between operations  0.64 us (1%)
    pallas_call x1, Pallas kernels, body(): pl.pallas_call(functools.partial(kernel, nf, ns), out_shape=(jax.ShapeDty...  45.1 us
    pallas_call x1, Pallas kernels, body(): pl.pallas_call(ship, out_shape=[jax.ShapeDtypeStruct(r.shape, r.dtype) fo...  0.95 us

profile of v1, /device:TPU:0, one launch (start us, length us, event | category | flops | bytes accessed | tf_op | source)
XLA Modules:
  0.0 46.7 jit_solution(12421658159130360531)
XLA Ops:
  0.6 45.1 %shard_map.111 = (bf16[128,2048]{1,0:T(8,128)(2,1)S(1)}, bf16[128,512]{1,0:T(8,128)(2,1)S(1)}, bf16[128,512]{1,0:T(8,128)(2,1)S(1)}, f32[64,512]{1,0:T(8,128)S(1)}) custom-call(bf16[128,4096]{1,0:T(8,128)(2,1)} %bitcast.12, bf16[64,512]{1,0:T(8,128)(2,1)} %bitcast.17, f32[1,64]{1,0:T(1,128)} %bitcast.18, f32[1,64]{1,0:T(1,128)} %bitcast.19, ...), custom_call_target="tpu_custom_call" | custom-call | tf_op jit(solution)/shard_map/pallas_call | solution.py:1145
  45.7 1.0 %shard_map.112 = (bf16[128,2048]{1,0:T(8,128)(2,1)}, bf16[128,512]{1,0:T(8,128)(2,1)}, bf16[128,512]{1,0:T(8,128)(2,1)}, f32[64,512]{1,0:T(8,128)}) custom-call(bf16[128,2048]{1,0:T(8,128)(2,1)S(1)} %get-tuple-element.12.refs_0_, bf16[128,512]{1,0:T(8,128)(2,1)S(1)} %get-tuple-element.13.refs_1_, bf16[128,512]{1,0:T(8,128)(2,1)S(1)} %get-tuple-element.14.refs_2_, ...), custom_call_target="tpu_custom_call" | custom-call | tf_op jit(solution)/shard_map/pallas_call | solution.py:1161

commit v2 on v1

--- a/solution.py
+++ b/solution.py
@@ -31,6 +31,9 @@
 
 
 QUARTER = 128
+PIECE = 64
+AHEAD = 2
+LOG2_E = 1.4426950408889634
 
 
 def kernel(
@@ -84,14 +87,11 @@
     joint,
     grad_b,
     grad_c,
-    acc_b,
-    acc_c,
     col_t,
     xt_t,
     xc_t,
     ent_t,
-    z_early,
-    z_last,
+    z_recv,
     ag_ssem,
     ag_rsem,
     x_ssem,
@@ -114,6 +114,7 @@
     wide = x.shape[1] // groups
     size = wide // per
     quarters = wide // QUARTER
+    parts = wide // PIECE
     few = QUARTER // size
     bits = nf.bit_length() - 1
     last = groups - 1
@@ -123,7 +124,8 @@
             (1 - 2 * ((f // 2**j) % 2)) * 2**j for j in range(bits) if (m // 2**j) % 2
         )
 
-    far_first = sorted(range(1, nf), key=lambda m: -bin(m // 2).count("1"))
+    near_first = sorted(range(1, nf), key=lambda m: bin(m // 2).count("1"))
+    far_first = near_first[::-1]
 
     own_weight = pltpu.make_async_copy(weight_hbm, gathered.at[f], own_sem.at[0])
     own_weight.start()
@@ -205,17 +207,14 @@
             device_id_type=MESH,
         )
 
-    for g in range(groups):
-        for m in far_first:
-            weight_copy(g, m).start()
+    for m in far_first:
+        weight_copy(0, m).start()
     for load in loads[2:]:
         load.wait()
     own_tokens = pltpu.make_async_copy(
         tokens.at[:, span_of(f, rows)], gathered_x.at[span_of(f, length)], own_sem.at[1]
     )
     own_tokens.start()
-    for m in far_first:
-        token_copy(m).start()
 
     @pl.when(z == 0)
     def _():
@@ -238,171 +237,268 @@
         low = (value - high.astype(F32)).astype(BF16)
         return dot(ones, high, 1, 1) + dot(ones, low, 1, 1)
 
-    def strip(q, n=1):
-        return slice(q * QUARTER, (q + n) * QUARTER)
-
-    def forward_copy(g, q):
+    def part(p):
+        return slice(p * PIECE, (p + 1) * PIECE)
+
+    def strip(q):
+        return slice(q * QUARTER, (q + 1) * QUARTER)
+
+    def forward_copy(g, p):
         return pltpu.make_async_remote_copy(
-            src_ref=send_f.at[g, strip(q)],
-            dst_ref=entry.at[g, strip(q)],
-            send_sem=f_ssem.at[g, q],
-            recv_sem=f_rsem.at[g, q],
+            src_ref=send_f.at[g, part(p)],
+            dst_ref=entry.at[g, part(p)],
+            send_sem=f_ssem.at[g, p],
+            recv_sem=f_rsem.at[g, p],
             device_id={"seq": (z + 1) % ns},
             device_id_type=MESH,
         )
 
-    def backward_copy(g, q):
+    def backward_copy(g, p):
         return pltpu.make_async_remote_copy(
-            src_ref=send_b.at[g, strip(q)],
-            dst_ref=later.at[g, strip(q)],
-            send_sem=b_ssem.at[g, q],
-            recv_sem=b_rsem.at[g, q],
+            src_ref=send_b.at[g, part(p)],
+            dst_ref=later.at[g, part(p)],
+            send_sem=b_ssem.at[g, p],
+            recv_sem=b_rsem.at[g, p],
             device_id={"seq": (z + ns - 1) % ns},
             device_id_type=MESH,
         )
 
-    def prepare(g):
-        for m in range(1, nf):
-            weight_copy(g, m).wait_recv()
+    def thirds(value, axis):
+        high = value.astype(BF16)
+        rest = value - high.astype(F32)
+        middle = rest.astype(BF16)
+        low = (rest - middle.astype(F32)).astype(BF16)
+        return jnp.concatenate([high, middle, low], axis=axis)
+
+    def steps(g, product):
         mine = span_of(g, per)
-        weight = jnp.concatenate([gathered[own, mine] for own in range(nf)], axis=1)
-        rate = rate_t[mine]
-        raw = bias_t[mine] + dot(weight, tokens[...], 1, 1)
+        raw = bias_t[mine] + product
         step = jnp.maximum(raw, 0.0) + jnp.log1p(jnp.exp(-jnp.abs(raw)))
-        before = iota((length, length), 0) <= iota((length, length), 1)
-        cum = dot(-rate * step, before.astype(F32), precision=HIGH)
-        raw_t[mine] = raw
-        cum_t[mine] = cum
-        step_t[mine] = step
-        final = cum[:, length - 1 : length]
-        block = jnp.broadcast_to(jnp.exp(final), (per, STATE))
-        block_t[mine] = block
-        decay_g[g] = dot(spread_one, halves(block, 0), 0, 0)
+        before = iota((3 * length, length), 0) % length <= iota((3 * length, length), 1)
+        cum = dot(thirds(-LOG2_E * rate_t[mine] * step, 1), before.astype(BF16))
         both = jnp.concatenate([cum, step], axis=0).T
         cum_c = both[:, :per]
         step_c = both[:, per:]
         cum_g[g] = cum_c
         step_g[g] = step_c
-        scale = expand(step_c * jnp.exp(cum_c[length - 1 : length] - cum_c))
-        spread_st[g] = scale
+        raw_t[mine] = raw
+        cum_t[mine] = cum
+        step_t[mine] = step
+        block_t[mine] = jnp.broadcast_to(jnp.exp2(cum[:, length - 1 : length]), (per, STATE))
+        return cum_c, step_c
+
+    def gather(g):
+        for m in far_first:
+            weight_copy(g, m).start()
+
+    def prepare_first():
+        mine = span_of(0, per)
+        product = dot(gathered[f, mine], tokens[:, span_of(f, rows)], 1, 1)
+        for n, m in enumerate(near_first):
+            weight_copy(0, m).wait_recv()
+            if n == 0:
+                gather(1)
+            elif n == nf // 2:
+                gather(2)
+            own = partner(m)
+            product = product + dot(gathered[own, mine], tokens[:, span_of(own, rows)], 1, 1)
+        for g in range(3, groups):
+            gather(g)
+        return steps(0, product)
+
+    def prepare(g):
+        for m in near_first:
+            weight_copy(g, m).wait_recv()
+        mine = span_of(g, per)
+        weight = jnp.concatenate([gathered[own, mine] for own in range(nf)], axis=1)
+        steps(g, dot(weight, tokens[...], 1, 1))
+
+        @pl.when(g == 2)
+        def _():
+            for m in far_first:
+                token_copy(m).start()
+
+    def local(g, cum_c, step_c, opening=False):
+        scale = expand(step_c * jnp.exp2(cum_c[length - 1 : length] - cum_c))
         b = b_in[:, span_of(g, STATE)]
         c = c_out[:, span_of(g, STATE)]
         xs = (x[:, span_of(g, wide)].astype(F32) * scale).astype(BF16)
-        ds = (dy[:, span_of(g, wide)].astype(F32) * expand(jnp.exp(cum_c))).astype(BF16)
+        ds = (dy[:, span_of(g, wide)].astype(F32) * expand(jnp.exp2(cum_c))).astype(BF16)
+        state = dot(xs, b, 0, 0)
+        grad = dot(ds, c, 0, 0)
+        spread_st[g] = scale
         xs_g[g] = xs
         ds_g[g] = ds
-        state = dot(xs, b, 0, 0)
-        grad = dot(ds, c, 0, 0)
+
+        @pl.when(z == 0)
+        def _():
+            send_f[g] = state.astype(BF16)
+            if opening:
+                for p in range(AHEAD):
+                    forward_copy(g, p).start()
+
+        @pl.when(z == ns - 1)
+        def _():
+            send_b[g] = grad.astype(BF16)
+            if opening:
+                for p in range(AHEAD):
+                    backward_copy(g, p).start()
+
         state_loc[g] = state
         grad_loc[g] = grad
-
-        @pl.when(z == 0)
-        def _():
-            send_f[g] = state.astype(BF16)
-            for q in range(quarters):
-                forward_copy(g, q).start()
-
-        @pl.when(z == ns - 1)
-        def _():
-            send_b[g] = grad.astype(BF16)
-            for q in range(quarters):
-                backward_copy(g, q).start()
-
+        decay_g[g] = dot(spread_one, halves(block_t[span_of(g, per)], 0), 0, 0)
         spread_s[g] = expand(step_c)
         meet_g[g] = dot(b, c, 1, 1)
 
-    def chain_f(g, q):
+    def chain_f(g, p):
         @pl.when(z > 0)
         def _():
-            forward_copy(g, q).wait_recv()
+            forward_copy(g, p).wait_recv()
 
         @pl.when(jnp.logical_and(z > 0, z < ns - 1))
         def _():
-            s = strip(q)
+            s = part(p)
             send_f[g, s] = (decay_g[g, s] * entry[g, s].astype(F32) + state_loc[g, s]).astype(BF16)
-            forward_copy(g, q).start()
-
-    def chain_b(g, q):
+
+        @pl.when(z < ns - 1 if p >= AHEAD else (z < ns - 1) & ((z > 0) | (g > 0)))
+        def _():
+            forward_copy(g, p).start()
+
+    def chain_b(g, p):
         @pl.when(z < ns - 1)
         def _():
-            backward_copy(g, q).wait_recv()
+            backward_copy(g, p).wait_recv()
 
         @pl.when(jnp.logical_and(z > 0, z < ns - 1))
         def _():
-            s = strip(q)
+            s = part(p)
             send_b[g, s] = (decay_g[g, s] * later[g, s].astype(F32) + grad_loc[g, s]).astype(BF16)
-            backward_copy(g, q).start()
-
-    def columns(g, q, n=1):
-        return pl.ds(pl.multiple_of(g * wide + q * QUARTER, QUARTER), n * QUARTER)
-
-    def heavy(g, q):
-        x_q = x[:, columns(g, q)]
-        dy_q = dy[:, columns(g, q)]
+
+        @pl.when(z > 0 if p >= AHEAD else (z > 0) & ((z < ns - 1) | (g > 0)))
+        def _():
+            backward_copy(g, p).start()
+
+    def columns(g, q):
+        return pl.ds(pl.multiple_of(g * wide + q * QUARTER, QUARTER), QUARTER)
+
+    def heavy(g, q0, n):
         meet = meet_g[g]
         upper = iota((length, length), 0) <= iota((length, length), 1)
         lanes = iota((length, QUARTER), 1)
         cum_r = cum_t[span_of(g, per)]
         cum_l = cum_g[g]
         step_l = step_g[g]
-        total = jnp.zeros((length, length), F32) if q == 0 else joint[...]
-        sums = []
-        weights = []
-        masked = []
-        for j in range(few):
-            k = q * few + j
-            mine = lanes // size == j
-            pair = dot(jnp.where(mine, x_q, jnp.zeros_like(x_q)), dy_q, 1, 1)
-            spread = cum_r[k : k + 1] - cum_l[:, k : k + 1]
-            decay = jnp.exp(jnp.where(upper, spread, -1e30))
-            weights.append((decay * meet).astype(BF16))
-            masked.append(jnp.where(mine, dy_q, jnp.zeros_like(dy_q)))
-            scaled = decay * pair * step_l[:, k : k + 1]
-            total = total + scaled
-            sums.append(jnp.sum(scaled * meet, axis=0, keepdims=True))
-        passed = dot(jnp.concatenate(weights, axis=1), jnp.concatenate(masked, axis=0))
-        through[g, :, strip(q)] = spread_s[g, :, strip(q)] * passed
-        col_t[g, q] = jnp.concatenate(sums, axis=0)
-        xt_t[g, q] = head_sums(x_q.astype(F32) * passed)
-        if q < quarters - 1:
+        total = jnp.zeros((length, length), F32) if q0 == 0 else joint[...]
+        for q in range(q0, q0 + n):
+            x_q = x[:, columns(g, q)]
+            dy_q = dy[:, columns(g, q)]
+            sums = []
+            weights = []
+            masked = []
+            split = [jnp.where(lanes // size == j, x_q, jnp.zeros_like(x_q)) for j in range(few)]
+            pairs = dot(jnp.concatenate(split, axis=0), dy_q, 1, 1)
+            for j in range(few):
+                k = q * few + j
+                mine = lanes // size == j
+                pair = pairs[j * length : (j + 1) * length]
+                spread = cum_r[k : k + 1] - cum_l[:, k : k + 1]
+                decay = jnp.exp2(jnp.where(upper, spread, -1e30))
+                weights.append((decay * meet).astype(BF16))
+                masked.append(jnp.where(mine, dy_q, jnp.zeros_like(dy_q)))
+                scaled = decay * pair * step_l[:, k : k + 1]
+                total = total + scaled
+                sums.append(jnp.sum(scaled * meet, axis=0, keepdims=True))
+            passed = dot(jnp.concatenate(weights, axis=1), jnp.concatenate(masked, axis=0))
+            through[g, :, strip(q)] = spread_s[g, :, strip(q)] * passed
+            col_t[g, q] = jnp.concatenate(sums, axis=0)
+            xt_t[g, q] = head_sums(x_q.astype(F32) * passed)
+        if q0 + n < quarters:
             joint[...] = total
         else:
             total = total.astype(BF16)
             grad_b[g] = dot(total, c_out[:, span_of(g, STATE)])
             grad_c[g] = dot(total, b_in[:, span_of(g, STATE)], 0, 0)
 
-    def finish_f(g, q, n):
-        c = c_out[:, span_of(g, STATE)]
-        state = entry[g, strip(q, n)]
-        ds = ds_g[g, :, strip(q, n)]
-        sums = head_sums(ds.astype(F32) * dot(c, state, 1, 1))
-        for i in range(n):
-            ent_t[g, q + i] = sums[i * few : (i + 1) * few]
-        value = dot(ds, state)
-        if q > 0:
-            value = value + acc_c[...]
-        if q + n < quarters:
-            acc_c[...] = value
-        else:
-            out_c[:, span_of(g, STATE)] = (grad_c[g] + value).astype(BF16)
-
-    def finish_b(g, q, n):
-        b = b_in[:, span_of(g, STATE)]
-        grad = later[g, strip(q, n)]
-        carried = dot(b, grad, 1, 1)
-        sums = head_sums(x[:, columns(g, q, n)].astype(F32) * carried)
-        for i in range(n):
-            xc_t[g, q + i] = sums[i * few : (i + 1) * few]
-        out_x[:, columns(g, q, n)] = (
-            through[g, :, strip(q, n)] + spread_st[g, :, strip(q, n)] * carried
-        ).astype(BF16)
-        value = dot(xs_g[g, :, strip(q, n)], grad)
-        if q > 0:
-            value = value + acc_b[...]
-        if q + n < quarters:
-            acc_b[...] = value
-        else:
-            out_b[:, span_of(g, STATE)] = (grad_b[g] + value).astype(BF16)
+    def sums_f(g):
+        @pl.when(z == 0)
+        def _():
+            ent_t[span_of(g, per)] = jnp.zeros((per, length), F32)
+
+        @pl.when(z > 0)
+        def _():
+            read = dot(c_out[:, span_of(g, STATE)], entry[g], 1, 1)
+            ent_t[span_of(g, per)] = head_sums(ds_g[g].astype(F32) * read)
+
+    def sums_b(g):
+        @pl.when(z == ns - 1)
+        def _():
+            xc_t[span_of(g, per)] = jnp.zeros((per, length), F32)
+
+        @pl.when(z < ns - 1)
+        def _():
+            carried = dot(b_in[:, span_of(g, STATE)], later[g], 1, 1)
+            xc_t[span_of(g, per)] = head_sums(x[:, span_of(g, wide)].astype(F32) * carried)
+
+    def results_f(g):
+        columns = span_of(g, STATE)
+
+        @pl.when(z == 0)
+        def _():
+            out_c[:, columns] = grad_c[g].astype(BF16)
+
+        @pl.when(z > 0)
+        def _():
+            out_c[:, columns] = (grad_c[g] + dot(ds_g[g], entry[g])).astype(BF16)
+
+    def results_b(g):
+        columns = span_of(g, STATE)
+        channels = span_of(g, wide)
+
+        @pl.when(z == ns - 1)
+        def _():
+            out_x[:, channels] = through[g].astype(BF16)
+            out_b[:, columns] = grad_b[g].astype(BF16)
+
+        @pl.when(z < ns - 1)
+        def _():
+            grad = later[g]
+            carried = dot(b_in[:, columns], grad, 1, 1)
+            out_x[:, channels] = (through[g] + spread_st[g] * carried).astype(BF16)
+            out_b[:, columns] = (grad_b[g] + dot(xs_g[g], grad)).astype(BF16)
+
+    def finish_f(g):
+        columns = span_of(g, STATE)
+
+        @pl.when(z == 0)
+        def _():
+            ent_t[span_of(g, per)] = jnp.zeros((per, length), F32)
+            out_c[:, columns] = grad_c[g].astype(BF16)
+
+        @pl.when(z > 0)
+        def _():
+            state = entry[g]
+            ds = ds_g[g]
+            read = dot(c_out[:, columns], state, 1, 1)
+            ent_t[span_of(g, per)] = head_sums(ds.astype(F32) * read)
+            out_c[:, columns] = (grad_c[g] + dot(ds, state)).astype(BF16)
+
+    def finish_b(g):
+        columns = span_of(g, STATE)
+        channels = span_of(g, wide)
+
+        @pl.when(z == ns - 1)
+        def _():
+            xc_t[span_of(g, per)] = jnp.zeros((per, length), F32)
+            out_x[:, channels] = through[g].astype(BF16)
+            out_b[:, columns] = grad_b[g].astype(BF16)
+
+        @pl.when(z < ns - 1)
+        def _():
+            grad = later[g]
+            carried = dot(b_in[:, columns], grad, 1, 1)
+            xc_t[span_of(g, per)] = head_sums(x[:, channels].astype(F32) * carried)
+            out_x[:, channels] = (through[g] + spread_st[g] * carried).astype(BF16)
+            out_b[:, columns] = (grad_b[g] + dot(xs_g[g], grad)).astype(BF16)
 
     def post(g):
         mine = span_of(g, per)
@@ -417,14 +513,14 @@
             return jnp.concatenate([parts[g, q] for q in range(quarters)], axis=0)
 
         xt = stacked(xt_t)
-        tail_xc = jnp.exp(cum[:, length - 1 : length] - cum) * stacked(xc_t)
+        tail_xc = jnp.exp2(cum[:, length - 1 : length] - cum) * xc_t[mine]
         leaving = step * tail_xc
-        grad_cum = stacked(col_t) - step * xt + stacked(ent_t) - leaving
+        grad_cum = stacked(col_t) - step * xt + ent_t[mine] - leaving
         closing = block_t[mine, :1] * jnp.sum(crossing, axis=1, keepdims=True) + jnp.sum(
             leaving, axis=1, keepdims=True
         )
-        after = (iota((length, length), 0) >= iota((length, length), 1)).astype(F32)
-        grad_log = dot(grad_cum, after, precision=HIGH) + closing
+        after = iota((3 * length, length), 0) % length >= iota((3 * length, length), 1)
+        grad_log = dot(thirds(grad_cum, 1), after.astype(BF16)) + closing
         grad_raw = (xt + tail_xc - rate * grad_log) * jax.nn.sigmoid(raw_t[mine])
         gathered_r[f, mine] = grad_raw.astype(BF16)
         for m in far_first:
@@ -438,20 +534,40 @@
     def slot_step(tau, carry):
         gf = tau - z
         gb = tau - (ns - 1 - z)
-        for q in range(quarters):
-            pl.when(within(gf))(lambda: chain_f(gf, q))
-            pl.when(within(gb))(lambda: chain_b(gb, q))
-            if q == 0:
-                pl.when(tau + 1 < groups)(lambda: prepare(tau + 1))
-            pl.when(within(tau))(lambda: heavy(tau, q))
-            if (q + 1) % FINISH == 0:
-                at = q + 1 - FINISH
-                pl.when(within(gf))(lambda: finish_f(gf, at, FINISH))
-                pl.when(within(gb))(lambda: finish_b(gb, at, FINISH))
-        pl.when(within(tau - furthest))(lambda: post(tau - furthest))
+        whole = tau - furthest
+        half = quarters // 2
+        both = jnp.logical_and
+        lag = tau <= groups + 1
+        now = tau > groups
+        early = tau + 1 < groups
+        edge = furthest == ns - 1
+        first = jnp.where(edge | (tau < 2), tau, jnp.where(tau == 2, -1, tau - 1))
+        second = jnp.where(edge | (tau < 1), tau, jnp.where(tau == 1, -1, tau - 1))
+        stride = parts // 4
+        for p in range(parts):
+            pl.when(within(gf))(lambda: chain_f(gf, p))
+            pl.when(within(gb))(lambda: chain_b(gb, p))
+            if p == stride - 1:
+                pl.when(early)(lambda: prepare(tau + 1))
+                pl.when(within(gf - 1) & lag & (tau + 1 >= groups))(lambda: finish_f(gf - 1))
+            elif p == 2 * stride - 1:
+                pl.when(within(first))(lambda: heavy(first, 0, half))
+                pl.when(within(gf - 1) & early)(lambda: finish_f(gf - 1))
+            elif p == 3 * stride - 1:
+                pl.when(early)(lambda: local(tau + 1, cum_g[tau + 1], step_g[tau + 1]))
+                pl.when(both(within(gb - 1), lag))(lambda: finish_b(gb - 1))
+                pl.when(both(within(whole - 1), lag))(lambda: post(whole - 1))
+            elif p == 4 * stride - 1:
+                pl.when(within(second))(lambda: heavy(second, half, quarters - half))
+        pl.when(both(within(gf), now))(lambda: sums_f(gf))
+        pl.when(both(within(gb), now))(lambda: sums_b(gb))
+        pl.when(both(within(whole), now))(lambda: post(whole))
+        pl.when(both(within(gf), now))(lambda: results_f(gf))
+        pl.when(both(within(gb), now))(lambda: results_b(gb))
         return carry
 
-    lax.fori_loop(-1, groups + ns - 1, slot_step, 0)
+    local(0, *prepare_first(), opening=True)
+    lax.fori_loop(0, groups + ns - 1, slot_step, 0)
 
     def product(first, count):
         raws = jnp.concatenate(
@@ -459,12 +575,22 @@
         )
         return dot(raws, gathered_x[...]).astype(BF16)
 
-    def exchange(target, n):
+    own_tokens.wait()
+    for m in range(1, nf):
+        token_copy(m).wait_recv()
+    shares = []
+    for n, (first, count) in enumerate(((0, groups - 2), (groups - 2, 1), (groups - 1, 1))):
+        for g in range(first, first + count):
+            for m in range(1, nf):
+                raw_copy(g, m).wait_recv()
+        place = slice(first * per, (first + count) * per)
+        z_recv[z, place] = product(first, count)
         copies = []
         for d in range(1, ns):
+            share = z_recv.at[z, place]
             copy = pltpu.make_async_remote_copy(
-                src_ref=target.at[z],
-                dst_ref=target.at[z],
+                src_ref=share,
+                dst_ref=share,
                 send_sem=z_ssem.at[n, d - 1],
                 recv_sem=z_rsem.at[n, d - 1],
                 device_id={"seq": (z + d) % ns},
@@ -472,31 +598,7 @@
             )
             copy.start()
             copies.append(copy)
-        return copies
-
-    own_tokens.wait()
-    for m in range(1, nf):
-        token_copy(m).wait_recv()
-    for g in range(last):
-        for m in range(1, nf):
-            raw_copy(g, m).wait_recv()
-    z_early[z] = product(0, last)
-    early = exchange(z_early, 0)
-    for m in range(1, nf):
-        raw_copy(last, m).wait_recv()
-    z_last[z] = product(last, 1)
-    late = exchange(z_last, 1)
-    for copies, source, place in (
-        (early, z_early, slice(0, last * per)),
-        (late, z_last, slice(last * per, heads)),
-    ):
-        for copy in copies:
-            copy.wait()
-        summed = source[0].astype(F32)
-        for k in range(1, ns):
-            summed = summed + source[k].astype(F32)
-        out_w[place] = summed
-
+        shares.append((place, copies))
     for m in range(1, nf):
         token_copy(m).wait_send()
         for g in range(groups):
@@ -506,14 +608,26 @@
     @pl.when(z < ns - 1)
     def _():
         for g in range(groups):
-            for q in range(quarters):
-                forward_copy(g, q).wait_send()
+            for p in range(parts):
+                forward_copy(g, p).wait_send()
 
     @pl.when(z > 0)
     def _():
         for g in range(groups):
-            for q in range(quarters):
-                backward_copy(g, q).wait_send()
+            for p in range(parts):
+                backward_copy(g, p).wait_send()
+
+    for place, copies in shares:
+        for copy in copies:
+            copy.wait_recv()
+        summed = z_recv[0, place].astype(F32)
+        for k in range(1, ns):
+            summed = summed + z_recv[k, place].astype(F32)
+        out_w[place] = summed
+
+    for _, copies in shares:
+        for copy in copies:
+            copy.wait_send()
 
 
 def ship(*refs):
@@ -1052,9 +1166,6 @@
     return (out_x[None], out_b[None], out_c[None], out_w.T)
 
 
-FINISH = 2
-
-
 def body(
     layer_input, dt_weight, dt_bias, decay_rate, ssm_input, in_basis, out_basis, out_cotangent
 ):
@@ -1067,6 +1178,7 @@
     wide = full // groups
     size = wide // per
     quarters = wide // QUARTER
+    parts = wide // PIECE
     few = QUARTER // size
     tall = (groups, wide, STATE)
     flat = (groups, length, wide)
@@ -1109,26 +1221,23 @@
         v((length, length), F32),
         v((groups, length, STATE), F32),
         v((groups, length, STATE), F32),
-        v((length, STATE), F32),
-        v((length, STATE), F32),
         v((groups, quarters, few, length), F32),
         v((groups, quarters, few, length), F32),
-        v((groups, quarters, few, length), F32),
-        v((groups, quarters, few, length), F32),
-        v((ns, heads - per, rows), BF16),
-        v((ns, per, rows), BF16),
+        v((heads, length), F32),
+        v((heads, length), F32),
+        v((ns, heads, rows), BF16),
         dma((groups, nf - 1)),
         dma((groups, nf - 1)),
         dma((nf - 1,)),
         dma((nf - 1,)),
         dma((groups, nf - 1)),
         dma((groups, nf - 1)),
-        dma((groups, quarters)),
-        dma((groups, quarters)),
-        dma((groups, quarters)),
-        dma((groups, quarters)),
-        dma((2, ns - 1)),
-        dma((2, ns - 1)),
+        dma((groups, parts)),
+        dma((groups, parts)),
+        dma((groups, parts)),
+        dma((groups, parts)),
+        dma((3, ns - 1)),
+        dma((3, ns - 1)),
     ]
     inside = pl.BlockSpec(memory_space=pltpu.VMEM)
     outside = pl.BlockSpec(memory_space=pltpu.HBM)
@@ -1177,7 +1286,8 @@
         nf = lax.axis_size("fsdp")
         shard = args[1].shape[0]
         lanes = args[4].shape[2] * STATE // args[5].shape[2]
-        fits = shard % 128 == 0 and nf & (nf - 1) == 0 and lanes % QUARTER == 0
+        several = args[5].shape[2] // STATE > 2
+        fits = several and shard % 128 == 0 and nf & (nf - 1) == 0 and lanes % (2 * QUARTER) == 0
         return (body if fits else general_body)(*args)
 
     return jax.shard_map(

time: 46.8 us -> 44.3 us (0.947)
  Pallas kernels: 46 us -> 43.5 us
    pallas_call x1, Pallas kernels: 45.1 us -> 42.5 us  [body(): pl.pallas_call(functools.partial(kernel, nf, ns), out_shape=(jax.ShapeDty...]
where the time goes in v2:
time: 44.3 us; the launch traced here: 44.1 us
  Pallas kernels  43.5 us (98%)
  between operations  0.64 us (1%)
    pallas_call x1, Pallas kernels, body(): pl.pallas_call(functools.partial(kernel, nf, ns), out_shape=(jax.ShapeDty...  42.5 us
    pallas_call x1, Pallas kernels, body(): pl.pallas_call(ship, out_shape=[jax.ShapeDtypeStruct(r.shape, r.dtype) fo...  0.95 us

profile of v2, /device:TPU:0, one launch (start us, length us, event | category | flops | bytes accessed | tf_op | source)
XLA Modules:
  0.0 44.1 jit_solution(16021053337746029868)
XLA Ops:
  0.6 42.5 %shard_map.111 = (bf16[128,2048]{1,0:T(8,128)(2,1)S(1)}, bf16[128,512]{1,0:T(8,128)(2,1)S(1)}, bf16[128,512]{1,0:T(8,128)(2,1)S(1)}, f32[64,512]{1,0:T(8,128)S(1)}) custom-call(bf16[128,4096]{1,0:T(8,128)(2,1)} %bitcast.12, bf16[64,512]{1,0:T(8,128)(2,1)} %bitcast.17, f32[1,64]{1,0:T(1,128)} %bitcast.18, f32[1,64]{1,0:T(1,128)} %bitcast.19, ...), custom_call_target="tpu_custom_call" | custom-call | tf_op jit(solution)/shard_map/pallas_call | solution.py:1254
  43.2 1.0 %shard_map.112 = (bf16[128,2048]{1,0:T(8,128)(2,1)}, bf16[128,512]{1,0:T(8,128)(2,1)}, bf16[128,512]{1,0:T(8,128)(2,1)}, f32[64,512]{1,0:T(8,128)}) custom-call(bf16[128,2048]{1,0:T(8,128)(2,1)S(1)} %get-tuple-element.12.refs_0_, bf16[128,512]{1,0:T(8,128)(2,1)S(1)} %get-tuple-element.13.refs_1_, bf16[128,512]{1,0:T(8,128)(2,1)S(1)} %get-tuple-element.14.refs_2_, ...), custom_call_target="tpu_custom_call" | custom-call | tf_op jit(solution)/shard_map/pallas_call | solution.py:1270

commit v3 on v2

--- a/solution.py
+++ b/solution.py
@@ -31,8 +31,8 @@
 
 
 QUARTER = 128
-PIECE = 64
-AHEAD = 2
+PIECE = 128
+AHEAD = 1
 LOG2_E = 1.4426950408889634
 
 
@@ -315,7 +315,12 @@
 
         @pl.when(g == 2)
         def _():
-            for m in far_first:
+            for m in near_first[: nf // 2]:
+                token_copy(m).start()
+
+        @pl.when(g == 3)
+        def _():
+            for m in near_first[nf // 2 :]:
                 token_copy(m).start()
 
     def local(g, cum_c, step_c, opening=False):
@@ -419,59 +424,33 @@
             grad_b[g] = dot(total, c_out[:, span_of(g, STATE)])
             grad_c[g] = dot(total, b_in[:, span_of(g, STATE)], 0, 0)
 
-    def sums_f(g):
-        @pl.when(z == 0)
-        def _():
-            ent_t[span_of(g, per)] = jnp.zeros((per, length), F32)
-
-        @pl.when(z > 0)
-        def _():
-            read = dot(c_out[:, span_of(g, STATE)], entry[g], 1, 1)
-            ent_t[span_of(g, per)] = head_sums(ds_g[g].astype(F32) * read)
-
-    def sums_b(g):
-        @pl.when(z == ns - 1)
-        def _():
-            xc_t[span_of(g, per)] = jnp.zeros((per, length), F32)
-
-        @pl.when(z < ns - 1)
-        def _():
-            carried = dot(b_in[:, span_of(g, STATE)], later[g], 1, 1)
-            xc_t[span_of(g, per)] = head_sums(x[:, span_of(g, wide)].astype(F32) * carried)
+    def store_sums(target, g, q, sums):
+        for i in range(sums.shape[0] // few):
+            target[g, q + i] = sums[i * few : (i + 1) * few]
+
+    def sums_f(g, q):
+        read = dot(c_out[:, span_of(g, STATE)], entry[g, strip(q)], 1, 1)
+        store_sums(ent_t, g, q, head_sums(ds_g[g, :, strip(q)].astype(F32) * read))
+
+    def sums_b(g, q):
+        carried = dot(b_in[:, span_of(g, STATE)], later[g, strip(q)], 1, 1)
+        store_sums(xc_t, g, q, head_sums(x[:, columns(g, q)].astype(F32) * carried))
 
     def results_f(g):
-        columns = span_of(g, STATE)
-
-        @pl.when(z == 0)
-        def _():
-            out_c[:, columns] = grad_c[g].astype(BF16)
-
-        @pl.when(z > 0)
-        def _():
-            out_c[:, columns] = (grad_c[g] + dot(ds_g[g], entry[g])).astype(BF16)
+        out_c[:, span_of(g, STATE)] = (grad_c[g] + dot(ds_g[g], entry[g])).astype(BF16)
 
     def results_b(g):
-        columns = span_of(g, STATE)
         channels = span_of(g, wide)
-
-        @pl.when(z == ns - 1)
-        def _():
-            out_x[:, channels] = through[g].astype(BF16)
-            out_b[:, columns] = grad_b[g].astype(BF16)
-
-        @pl.when(z < ns - 1)
-        def _():
-            grad = later[g]
-            carried = dot(b_in[:, columns], grad, 1, 1)
-            out_x[:, channels] = (through[g] + spread_st[g] * carried).astype(BF16)
-            out_b[:, columns] = (grad_b[g] + dot(xs_g[g], grad)).astype(BF16)
+        carried = dot(b_in[:, span_of(g, STATE)], later[g], 1, 1)
+        out_x[:, channels] = (through[g] + spread_st[g] * carried).astype(BF16)
+        out_b[:, span_of(g, STATE)] = (grad_b[g] + dot(xs_g[g], later[g])).astype(BF16)
 
     def finish_f(g):
         columns = span_of(g, STATE)
 
         @pl.when(z == 0)
         def _():
-            ent_t[span_of(g, per)] = jnp.zeros((per, length), F32)
+            ent_t[g] = jnp.zeros((quarters, few, length), F32)
             out_c[:, columns] = grad_c[g].astype(BF16)
 
         @pl.when(z > 0)
@@ -479,7 +458,7 @@
             state = entry[g]
             ds = ds_g[g]
             read = dot(c_out[:, columns], state, 1, 1)
-            ent_t[span_of(g, per)] = head_sums(ds.astype(F32) * read)
+            store_sums(ent_t, g, 0, head_sums(ds.astype(F32) * read))
             out_c[:, columns] = (grad_c[g] + dot(ds, state)).astype(BF16)
 
     def finish_b(g):
@@ -488,7 +467,7 @@
 
         @pl.when(z == ns - 1)
         def _():
-            xc_t[span_of(g, per)] = jnp.zeros((per, length), F32)
+            xc_t[g] = jnp.zeros((quarters, few, length), F32)
             out_x[:, channels] = through[g].astype(BF16)
             out_b[:, columns] = grad_b[g].astype(BF16)
 
@@ -496,7 +475,7 @@
         def _():
             grad = later[g]
             carried = dot(b_in[:, columns], grad, 1, 1)
-            xc_t[span_of(g, per)] = head_sums(x[:, channels].astype(F32) * carried)
+            store_sums(xc_t, g, 0, head_sums(x[:, channels].astype(F32) * carried))
             out_x[:, channels] = (through[g] + spread_st[g] * carried).astype(BF16)
             out_b[:, columns] = (grad_b[g] + dot(xs_g[g], grad)).astype(BF16)
 
@@ -513,9 +492,9 @@
             return jnp.concatenate([parts[g, q] for q in range(quarters)], axis=0)
 
         xt = stacked(xt_t)
-        tail_xc = jnp.exp2(cum[:, length - 1 : length] - cum) * xc_t[mine]
+        tail_xc = jnp.exp2(cum[:, length - 1 : length] - cum) * stacked(xc_t)
         leaving = step * tail_xc
-        grad_cum = stacked(col_t) - step * xt + ent_t[mine] - leaving
+        grad_cum = stacked(col_t) - step * xt + stacked(ent_t) - leaving
         closing = block_t[mine, :1] * jnp.sum(crossing, axis=1, keepdims=True) + jnp.sum(
             leaving, axis=1, keepdims=True
         )
@@ -536,34 +515,53 @@
         gb = tau - (ns - 1 - z)
         whole = tau - furthest
         half = quarters // 2
-        both = jnp.logical_and
-        lag = tau <= groups + 1
-        now = tau > groups
         early = tau + 1 < groups
         edge = furthest == ns - 1
+        lag = tau <= groups + 1
+        now = (tau > groups) & ~edge
+        at_front = (z == 0) & (tau > groups) & within(gb)
+        at_back = (z == ns - 1) & (tau > groups) & within(gf)
         first = jnp.where(edge | (tau < 2), tau, jnp.where(tau == 2, -1, tau - 1))
         second = jnp.where(edge | (tau < 1), tau, jnp.where(tau == 1, -1, tau - 1))
+        done_f = gf - 1
+        done_b = gb - 1
+        done = whole - 1
         stride = parts // 4
         for p in range(parts):
             pl.when(within(gf))(lambda: chain_f(gf, p))
             pl.when(within(gb))(lambda: chain_b(gb, p))
+            if (p + 1) % (parts // quarters) == 0 and p + 1 < parts:
+                q = p * quarters // parts
+                pl.when(at_front)(lambda: sums_b(gb, q))
+                pl.when(at_back)(lambda: sums_f(gf, q))
             if p == stride - 1:
                 pl.when(early)(lambda: prepare(tau + 1))
-                pl.when(within(gf - 1) & lag & (tau + 1 >= groups))(lambda: finish_f(gf - 1))
+                pl.when(within(done_f) & lag & ~early)(lambda: finish_f(done_f))
             elif p == 2 * stride - 1:
                 pl.when(within(first))(lambda: heavy(first, 0, half))
-                pl.when(within(gf - 1) & early)(lambda: finish_f(gf - 1))
+                pl.when(within(done_f) & early)(lambda: finish_f(done_f))
             elif p == 3 * stride - 1:
                 pl.when(early)(lambda: local(tau + 1, cum_g[tau + 1], step_g[tau + 1]))
-                pl.when(both(within(gb - 1), lag))(lambda: finish_b(gb - 1))
-                pl.when(both(within(whole - 1), lag))(lambda: post(whole - 1))
+                pl.when(within(done_b) & lag)(lambda: finish_b(done_b))
+                pl.when(within(done) & lag)(lambda: post(done))
             elif p == 4 * stride - 1:
                 pl.when(within(second))(lambda: heavy(second, half, quarters - half))
-        pl.when(both(within(gf), now))(lambda: sums_f(gf))
-        pl.when(both(within(gb), now))(lambda: sums_b(gb))
-        pl.when(both(within(whole), now))(lambda: post(whole))
-        pl.when(both(within(gf), now))(lambda: results_f(gf))
-        pl.when(both(within(gb), now))(lambda: results_b(gb))
+
+        @pl.when(at_front)
+        def _():
+            sums_b(gb, quarters - 1)
+            post(gb)
+            results_b(gb)
+
+        @pl.when(at_back)
+        def _():
+            sums_f(gf, quarters - 1)
+            post(gf)
+            results_f(gf)
+
+        pl.when(now & within(gf))(lambda: finish_f(gf))
+        pl.when(now & within(gb))(lambda: finish_b(gb))
+        pl.when(now & within(whole))(lambda: post(whole))
         return carry
 
     local(0, *prepare_first(), opening=True)
@@ -573,18 +571,31 @@
         raws = jnp.concatenate(
             [gathered_r[own, first * per : (first + count) * per] for own in range(nf)], axis=1
         )
-        return dot(raws, gathered_x[...]).astype(BF16)
+        return dot(raws, gathered_x[...])
+
+    def product_as_they_come(g):
+        def term(own):
+            return dot(gathered_r[own, span_of(g, per)], gathered_x[span_of(own, length)])
+
+        total = term(f)
+        for m in near_first:
+            raw_copy(g, m).wait_recv()
+            total = total + term(partner(m))
+        return total
 
     own_tokens.wait()
     for m in range(1, nf):
         token_copy(m).wait_recv()
     shares = []
     for n, (first, count) in enumerate(((0, groups - 2), (groups - 2, 1), (groups - 1, 1))):
-        for g in range(first, first + count):
-            for m in range(1, nf):
-                raw_copy(g, m).wait_recv()
         place = slice(first * per, (first + count) * per)
-        z_recv[z, place] = product(first, count)
+        if first == last:
+            z_recv[z, place] = product_as_they_come(last).astype(BF16)
+        else:
+            for g in range(first, first + count):
+                for m in range(1, nf):
+                    raw_copy(g, m).wait_recv()
+            z_recv[z, place] = product(first, count).astype(BF16)
         copies = []
         for d in range(1, ns):
             share = z_recv.at[z, place]
@@ -1223,8 +1234,8 @@
         v((groups, length, STATE), F32),
         v((groups, quarters, few, length), F32),
         v((groups, quarters, few, length), F32),
-        v((heads, length), F32),
-        v((heads, length), F32),
+        v((groups, quarters, few, length), F32),
+        v((groups, quarters, few, length), F32),
         v((ns, heads, rows), BF16),
         dma((groups, nf - 1)),
         dma((groups, nf - 1)),

time: 44.3 us -> 43.6 us (0.984)
  Pallas kernels: 43.5 us -> 42.8 us
    pallas_call x1, Pallas kernels: 42.5 us -> 41.9 us  [body(): pl.pallas_call(functools.partial(kernel, nf, ns), out_shape=(jax.ShapeDty...]
where the time goes in v3:
time: 43.6 us; the launch traced here: 43.4 us
  Pallas kernels  42.8 us (98%)
  between operations  0.64 us (1%)
    pallas_call x1, Pallas kernels, body(): pl.pallas_call(functools.partial(kernel, nf, ns), out_shape=(jax.ShapeDty...  41.9 us
    pallas_call x1, Pallas kernels, body(): pl.pallas_call(ship, out_shape=[jax.ShapeDtypeStruct(r.shape, r.dtype) fo...  0.95 us

profile of v3, /device:TPU:0, one launch (start us, length us, event | category | flops | bytes accessed | tf_op | source)
XLA Modules:
  0.0 43.4 jit_solution(1283780942781029974)
XLA Ops:
  0.6 41.9 %shard_map.111 = (bf16[128,2048]{1,0:T(8,128)(2,1)S(1)}, bf16[128,512]{1,0:T(8,128)(2,1)S(1)}, bf16[128,512]{1,0:T(8,128)(2,1)S(1)}, f32[64,512]{1,0:T(8,128)S(1)}) custom-call(bf16[128,4096]{1,0:T(8,128)(2,1)} %bitcast.12, bf16[64,512]{1,0:T(8,128)(2,1)} %bitcast.17, f32[1,64]{1,0:T(1,128)} %bitcast.18, f32[1,64]{1,0:T(1,128)} %bitcast.19, ...), custom_call_target="tpu_custom_call" | custom-call | tf_op jit(solution)/shard_map/pallas_call | solution.py:1265
  42.5 1.0 %shard_map.112 = (bf16[128,2048]{1,0:T(8,128)(2,1)}, bf16[128,512]{1,0:T(8,128)(2,1)}, bf16[128,512]{1,0:T(8,128)(2,1)}, f32[64,512]{1,0:T(8,128)}) custom-call(bf16[128,2048]{1,0:T(8,128)(2,1)S(1)} %get-tuple-element.12.refs_0_, bf16[128,512]{1,0:T(8,128)(2,1)S(1)} %get-tuple-element.13.refs_1_, bf16[128,512]{1,0:T(8,128)(2,1)S(1)} %get-tuple-element.14.refs_2_, ...), custom_call_target="tpu_custom_call" | custom-call | tf_op jit(solution)/shard_map/pallas_call | solution.py:1281

commit v4 on v3

--- a/solution.py
+++ b/solution.py
@@ -587,7 +587,7 @@
     for m in range(1, nf):
         token_copy(m).wait_recv()
     shares = []
-    for n, (first, count) in enumerate(((0, groups - 2), (groups - 2, 1), (groups - 1, 1))):
+    for n, (first, count) in enumerate(((0, 1), (1, groups - 3), (groups - 2, 1), (groups - 1, 1))):
         place = slice(first * per, (first + count) * per)
         if first == last:
             z_recv[z, place] = product_as_they_come(last).astype(BF16)
@@ -1247,8 +1247,8 @@
         dma((groups, parts)),
         dma((groups, parts)),
         dma((groups, parts)),
-        dma((3, ns - 1)),
-        dma((3, ns - 1)),
+        dma((4, ns - 1)),
+        dma((4, ns - 1)),
     ]
     inside = pl.BlockSpec(memory_space=pltpu.VMEM)
     outside = pl.BlockSpec(memory_space=pltpu.HBM)
@@ -1297,7 +1297,7 @@
         nf = lax.axis_size("fsdp")
         shard = args[1].shape[0]
         lanes = args[4].shape[2] * STATE // args[5].shape[2]
-        several = args[5].shape[2] // STATE > 2
+        several = args[5].shape[2] // STATE > 3
         fits = several and shard % 128 == 0 and nf & (nf - 1) == 0 and lanes % (2 * QUARTER) == 0
         return (body if fits else general_body)(*args)
 

time: 43.6 us -> 43.3 us (level)
  no operation moved by 1% of the time
where the time goes in v4:
time: 43.3 us; the launch traced here: 43.2 us
  Pallas kernels  42.5 us (98%)
  between operations  0.64 us (1%)
    pallas_call x1, Pallas kernels, body(): pl.pallas_call(functools.partial(kernel, nf, ns), out_shape=(jax.ShapeDty...  41.6 us
    pallas_call x1, Pallas kernels, body(): pl.pallas_call(ship, out_shape=[jax.ShapeDtypeStruct(r.shape, r.dtype) fo...  0.95 us

profile of v4, /device:TPU:0, one launch (start us, length us, event | category | flops | bytes accessed | tf_op | source)
XLA Modules:
  0.0 43.2 jit_solution(8043428710953077706)
XLA Ops:
  0.6 41.6 %shard_map.111 = (bf16[128,2048]{1,0:T(8,128)(2,1)S(1)}, bf16[128,512]{1,0:T(8,128)(2,1)S(1)}, bf16[128,512]{1,0:T(8,128)(2,1)S(1)}, f32[64,512]{1,0:T(8,128)S(1)}) custom-call(bf16[128,4096]{1,0:T(8,128)(2,1)} %bitcast.12, bf16[64,512]{1,0:T(8,128)(2,1)} %bitcast.17, f32[1,64]{1,0:T(1,128)} %bitcast.18, f32[1,64]{1,0:T(1,128)} %bitcast.19, ...), custom_call_target="tpu_custom_call" | custom-call | tf_op jit(solution)/shard_map/pallas_call | solution.py:1265
  42.2 1.0 %shard_map.112 = (bf16[128,2048]{1,0:T(8,128)(2,1)}, bf16[128,512]{1,0:T(8,128)(2,1)}, bf16[128,512]{1,0:T(8,128)(2,1)}, f32[64,512]{1,0:T(8,128)}) custom-call(bf16[128,2048]{1,0:T(8,128)(2,1)S(1)} %get-tuple-element.12.refs_0_, bf16[128,512]{1,0:T(8,128)(2,1)S(1)} %get-tuple-element.13.refs_1_, bf16[128,512]{1,0:T(8,128)(2,1)S(1)} %get-tuple-element.14.refs_2_, ...), custom_call_target="tpu_custom_call" | custom-call | tf_op jit(solution)/shard_map/pallas_call | solution.py:1281
